TPU v7x, 32 devices: a whole 2x2x4 slice. The times are simulated.
32 devices in a mesh: gx: 8 (over z, y), gy: 4 (over x, core).
Axes of the slice: x: 2, y: 2, z: 4, core: 2. Of those that a mesh axis runs over, the one named last changes fastest.
Arguments:
- image_feats: bfloat16 [16384, 4096], P('gx', 'gy'), may hold values from -6 to 6
- w_kv: bfloat16 [4096, 2048], P('gy'), may hold values from -0.09375 to 0.09375
- k_gain: float32 [128], replicated, may hold values from 0.25 to 1.75
- tile_rows: int32 [128], replicated, may hold values from 0 to 128
- deal: int32 [8, 16], replicated, may hold values from 0 to 127, as said below
Outputs:
- keys_out: bfloat16 [16384, 1024], P('gx', 'gy')
- values_out: bfloat16 [16384, 1024], P('gx', 'gy')
Inputs may be any that keep to these rules, and one draw needn't show every extreme that they name: Each input tile is named exactly once; deal[j, s] % 16 == s; two entries of one row j that name tiles of the same index of gx stand in columns s that differ by a multiple of 8, so one row names at most 2 tiles of one index of gx, and exactly 2 for some.
All inputs are finite; a program needn't handle non-finite values.
Results may differ from a plain program's by a relative error of at most 0.001.
Values may be sent and summed in bfloat16 or wider, within the bound.
A program may use at most 128 MiB of HBM per device.

v0:
```python
import functools

import jax
import jax.numpy as jnp
from jax import lax
from jax.experimental import pallas as pl
from jax.experimental.pallas import tpu as pltpu
from jax.sharding import PartitionSpec as P

HD = 128
TILE = 128
TPD = 16


epsilon = 1e-05


def plain_local(image_feats, w_kv, k_gain, tile_rows, deal):
    local_width = image_feats.shape[1]
    groups = lax.axis_size("gx")
    own_index = lax.axis_index("gx")
    slots = max(1, TPD // groups)
    wanted = lax.dynamic_index_in_dim(deal, own_index, 0, keepdims=False)
    slot_index = jnp.arange(TPD, dtype=jnp.int32)
    slot_class = slot_index // groups
    places = jnp.arange(slots, dtype=jnp.int32)
    class_match = slot_class[None, :] == places[:, None]
    own_tiles = own_index * TPD + slot_index
    sending = deal == own_tiles[None, :]
    send_select = (sending[:, None, :] & class_match[None, :, :]).astype(jnp.bfloat16)
    blocks = image_feats.reshape(TPD, TILE, local_width)
    outgoing = jnp.einsum(
        "dcs,str->dctr", send_select, blocks, preferred_element_type=jnp.float32
    ).astype(jnp.bfloat16)
    incoming = lax.all_to_all(outgoing, "gx", split_axis=0, concat_axis=0, tiled=True)
    sources = jnp.arange(groups, dtype=jnp.int32)
    from_source = (wanted // TPD)[:, None] == sources[None, :]
    take_select = (from_source[:, :, None] & class_match.T[:, None, :]).astype(jnp.bfloat16)
    dealt_tiles = jnp.einsum(
        "snc,nctr->str", take_select, incoming, preferred_element_type=jnp.float32
    ).astype(jnp.bfloat16)
    row_count = TPD * TILE
    dealt_rows = dealt_tiles.reshape(row_count, local_width)
    total_kv = w_kv.shape[1] // 2
    partial_value = jnp.dot(dealt_rows, w_kv, preferred_element_type=jnp.float32)
    projected = lax.psum_scatter(
        partial_value.reshape(row_count, 2, total_kv), "gy", scatter_dimension=2, tiled=True
    )
    share_cols = projected.shape[2]
    key_pre = projected[:, 0, :].reshape(row_count, share_cols // HD, HD)
    value_pre = projected[:, 1, :]
    mean_square = jnp.mean(key_pre * key_pre, axis=-1, keepdims=True)
    normed = (key_pre * lax.rsqrt(mean_square + epsilon) * k_gain).reshape(row_count, share_cols)
    all_tiles = jnp.arange(tile_rows.shape[0], dtype=jnp.int32)
    limits = jnp.sum(
        jnp.where(wanted[:, None] == all_tiles[None, :], tile_rows[None, :], 0), axis=1
    )
    position = jnp.arange(TILE, dtype=jnp.int32)
    valid_rows = (position[None, :] < limits[:, None]).reshape(row_count, 1)
    keys_out = jnp.where(valid_rows, normed, 0.0).astype(jnp.bfloat16)
    values_out = jnp.where(valid_rows, value_pre, 0.0).astype(jnp.bfloat16)
    return (keys_out, values_out)


MESH = pl.DeviceIdType.MESH
PIECE = 16


def route(step, me, groups, slots):
    flips = groups - 1 - step // slots
    target, bit = 0, 1
    while bit < groups:
        target += (me // bit + flips // bit) % 2 * bit
        bit *= 2
    return target, step % slots


def tables(me, groups, slots, tile_rows, deal):
    per_tile = TILE // PIECE
    step = jnp.arange(TPD, dtype=jnp.int32)
    target, cls = route(step, me, groups, slots)
    column = jnp.arange(TPD, dtype=jnp.int32)
    row = jnp.arange(groups, dtype=jnp.int32)
    named = deal == (me * TPD + column)[None, :]
    chosen = (
        named[None] & (target[:, None] == row)[:, :, None]
        & (cls[:, None] == column // groups)[:, None, :]
    )
    slot = jnp.sum(jnp.where(chosen, column, 0), axis=(1, 2))
    own_rows = lax.dynamic_slice(tile_rows, (me * TPD,), (TPD,))
    limit = jnp.sum(jnp.where(slot[:, None] == column[None, :], own_rows[None, :], 0), axis=1)
    count = jnp.maximum((limit + PIECE - 1) // PIECE, 1)
    first = jnp.sum(jnp.where(step[None, :] < step[:, None], count[None, :], 0), axis=1)
    place = jnp.arange(TPD * per_tile, dtype=jnp.int32)[:, None]
    inside = (first[None, :] <= place) & (place < (first + count)[None, :])
    source = jnp.sum(
        jnp.where(inside, slot[None, :] * per_tile + place - first[None, :], 0), axis=1
    )
    part = jnp.arange(per_tile, dtype=jnp.int32)[None, :]
    piece = first[:, None] + jnp.minimum(part, count[:, None] - 1)
    return source, piece.reshape(-1), limit


def project_kernel(
    groups, slots, chunks, source_ref, piece_ref, limit_ref, gain_ref, feats_ref, w_ref, dealt_ref,
    natural, mine, theirs, w_mine, w_theirs, x_out, x_in, packed, done,
    load_sem, w_load_sem, w_send, w_recv, f_send, f_recv, x_send, x_recv, o_send, o_recv, own_sem,
):
    me = lax.axis_index("gx")
    place = lax.axis_index("gy")
    across = place // 2
    core = place % 2
    other_across, other_core = 1 - across, 1 - core
    core_mate = (me, across * 2 + other_core)
    x_mate = (me, other_across * 2 + core)
    share = w_mine.shape[2]
    total = w_ref.shape[1] // 2
    steps = groups * slots

    def columns(block, of_core):
        chip = other_across if block < 2 else across
        first = (block % 2) * total + (chip * 2 + of_core) * share
        return pl.ds(pl.multiple_of(first, 128), share)

    load = pltpu.make_async_copy(feats_ref, natural, load_sem)
    load.start()
    w_loads = [
        pltpu.make_async_copy(w_ref.at[:, columns(b, core)], w_mine.at[b], w_load_sem.at[b])
        for b in range(4)
    ]
    for copy in w_loads:
        copy.start()

    barrier = pltpu.get_barrier_semaphore()
    for mate in (core_mate, x_mate):
        pl.semaphore_signal(barrier, inc=1, device_id=mate, device_id_type=MESH)
    for ahead in range(1, groups):
        pl.semaphore_signal(
            barrier, inc=1, device_id=((me + ahead) % groups, place), device_id_type=MESH
        )
    pl.semaphore_wait(barrier, groups + 1)

    w_copies = [
        pltpu.make_async_remote_copy(
            src_ref=w_ref.at[:, columns(b, other_core)],
            dst_ref=w_theirs.at[b],
            send_sem=w_send.at[b],
            recv_sem=w_recv.at[b],
            device_id=core_mate,
            device_id_type=MESH,
        )
        for b in range(4)
    ]

    def f_copy(k):
        return pltpu.make_async_remote_copy(
            src_ref=mine.at[k], dst_ref=theirs.at[k], send_sem=f_send.at[k],
            recv_sem=f_recv.at[k], device_id=core_mate, device_id_type=MESH,
        )

    def x_copy(k):
        return pltpu.make_async_remote_copy(
            src_ref=x_out.at[k], dst_ref=x_in.at[k], send_sem=x_send.at[k],
            recv_sem=x_recv.at[k], device_id=x_mate, device_id_type=MESH,
        )

    def o_copy(k, target, landing):
        return pltpu.make_async_remote_copy(
            src_ref=done.at[k], dst_ref=dealt_ref.at[landing], send_sem=o_send.at[k],
            recv_sem=o_recv.at[landing], device_id=(target, place), device_id_type=MESH,
        )

    w_copies[0].start()
    w_copies[1].start()
    load.wait()

    def order(j, carry):
        for part in range(TILE // PIECE):
            mine[j, part * PIECE : (part + 1) * PIECE, :] = natural[
                source_ref[j * (TILE // PIECE) + part]
            ]
        f_copy(j).start()
        return carry

    lax.fori_loop(0, chunks, order, 0)
    w_copies[2].start()
    w_copies[3].start()

    def partial(k, block):
        return jnp.dot(
            mine[k], w_mine[block], preferred_element_type=jnp.float32
        ) + jnp.dot(theirs[k], w_theirs[block], preferred_element_type=jnp.float32)

    for b in range(2):
        w_loads[b].wait()
        w_copies[b].wait_recv()

    def outward(k, carry):
        f_copy(k).wait_recv()
        x_out[k, :, :share] = partial(k, 0)
        x_out[k, :, share:] = partial(k, 1)
        x_copy(k).start()
        return carry

    lax.fori_loop(0, chunks, outward, 0)
    for b in range(2, 4):
        w_loads[b].wait()
        w_copies[b].wait_recv()

    def finish(j):
        key_part = partial(j, 2)
        value_part = partial(j, 3)
        x_copy(j).wait_recv()
        key_pre = key_part + x_in[j, :, :share]
        value_pre = value_part + x_in[j, :, share:]
        parts = TILE // PIECE
        rows = pl.ds(j * parts, parts)
        for h in range(share // HD):
            head = slice(h * HD, (h + 1) * HD)
            one = key_pre[:, head]
            mean_square = jnp.mean(one * one, axis=-1, keepdims=True)
            normed = one * lax.rsqrt(mean_square + epsilon) * gain_ref[...]
            packed[rows, :, head] = normed.astype(jnp.bfloat16).reshape(parts, PIECE, HD)
        packed[rows, :, share:] = value_pre.astype(jnp.bfloat16).reshape(parts, PIECE, share)

    def assemble(k):
        position = lax.broadcasted_iota(jnp.int32, (PIECE, 2 * share), 0)
        limit = limit_ref[k]
        for part in range(TILE // PIECE):
            held = packed[piece_ref[k * (TILE // PIECE) + part]]
            kept = jnp.where(position < limit - part * PIECE, held.astype(jnp.float32), 0.0)
            done[k, part * PIECE : (part + 1) * PIECE, :] = kept.astype(jnp.bfloat16)

    def dispatch(k, carry):
        assemble(k)
        target, cls = route(k, me, groups, slots)
        o_copy(k, target, me * slots + cls).start()
        return carry

    def inward(k, carry):
        finish(k)
        return dispatch(k, carry)

    leaving = steps - slots
    together = min(chunks, leaving)
    lax.fori_loop(0, together, inward, 0)
    for j in range(together, chunks):
        finish(j)
    if together < leaving:
        lax.fori_loop(together, leaving, dispatch, 0)
    own = []
    for c in range(slots):
        k = leaving + c
        assemble(k)
        own.append(
            pltpu.make_async_copy(done.at[k], dealt_ref.at[me * slots + c], own_sem.at[c])
        )
        own[-1].start()

    for copy in w_copies:
        copy.wait_send()

    def drain(k, carry):
        f_copy(k).wait_send()
        x_copy(k).wait_send()
        return carry

    lax.fori_loop(0, chunks, drain, 0)

    def drain_out(k, carry):
        target, cls = route(k, me, groups, slots)
        o_copy(k, target, me * slots + cls).wait_send()
        o_copy(k, target, target * slots + cls).wait_recv()
        return carry

    lax.fori_loop(0, steps - slots, drain_out, 0)
    for copy in own:
        copy.wait()


def place_kernel(groups, slots, deal_ref, dealt_ref, keys_ref, values_ref, out_sem):
    me = lax.axis_index("gx")
    share = keys_ref.shape[1]
    stores = []
    for s in range(TPD):
        landing = deal_ref[me, s] // TPD * slots + s // groups
        for which, out in enumerate((keys_ref, values_ref)):
            stores.append(
                pltpu.make_async_copy(
                    dealt_ref.at[landing, :, pl.ds(which * share, share)],
                    out.at[pl.ds(s * TILE, TILE), :],
                    out_sem.at[which, s],
                )
            )
            stores[-1].start()
    for copy in stores:
        copy.wait()


def kernel_local(image_feats, w_kv, k_gain, tile_rows, deal):
    groups = lax.axis_size("gx")
    slots = TPD // groups
    width = image_feats.shape[1]
    share = w_kv.shape[1] // 2 // lax.axis_size("gy")
    steps = TPD
    bf16, f32 = jnp.bfloat16, jnp.float32
    smem = pl.BlockSpec(memory_space=pltpu.SMEM)
    anywhere = pl.BlockSpec(memory_space=pl.ANY)
    dma = pltpu.SemaphoreType.DMA

    def project(chunks, call):
        return pl.pallas_call(
            functools.partial(project_kernel, groups, slots, chunks),
            out_shape=jax.ShapeDtypeStruct((TPD, TILE, 2 * share), bf16),
            in_specs=[smem, smem, smem, pl.BlockSpec(memory_space=pltpu.VMEM), anywhere, anywhere],
            out_specs=anywhere,
            scratch_shapes=[
                pltpu.VMEM((TPD * TILE // PIECE, PIECE, width), bf16),
                pltpu.VMEM((chunks, TILE, width), bf16),
                pltpu.VMEM((chunks, TILE, width), bf16),
                pltpu.VMEM((4, width, share), bf16),
                pltpu.VMEM((4, width, share), bf16),
                pltpu.VMEM((chunks, TILE, 2 * share), f32),
                pltpu.VMEM((chunks, TILE, 2 * share), f32),
                pltpu.VMEM((chunks * TILE // PIECE, PIECE, 2 * share), bf16),
                pltpu.VMEM((steps, TILE, 2 * share), bf16),
                dma, dma((4,)), dma((4,)), dma((4,)), dma((chunks,)), dma((chunks,)),
                dma((chunks,)), dma((chunks,)), dma((steps,)), dma((steps,)), dma((slots,)),
            ],
            compiler_params=pltpu.CompilerParams(collective_id=call, has_side_effects=True),
            name=f"project_and_deal_{chunks}",
        )

    sizes = (TPD * 11 // 16, TPD * 3 // 4, TPD)
    pieces = jnp.maximum((tile_rows + PIECE - 1) // PIECE, 1).reshape(groups, TPD)
    fullest = jnp.max(jnp.sum(pieces, axis=1))
    branch = sum((fullest > size * (TILE // PIECE)).astype(jnp.int32) for size in sizes[:-1])
    dealt = lax.switch(
        branch,
        [project(size, call) for call, size in enumerate(sizes)],
        *tables(lax.axis_index("gx"), groups, slots, tile_rows, deal),
        k_gain.reshape(1, HD), image_feats.reshape(-1, PIECE, width), w_kv,
    )
    result = jax.ShapeDtypeStruct((TPD * TILE, share), bf16)
    return pl.pallas_call(
        functools.partial(place_kernel, groups, slots),
        out_shape=(result, result),
        in_specs=[smem, pl.BlockSpec(memory_space=pltpu.VMEM)],
        out_specs=(anywhere, anywhere),
        scratch_shapes=[dma((2, TPD))],
        name="place_tiles",
    )(deal, dealt)


def solution(mesh):
    groups, width_parts = mesh.shape["gx"], mesh.shape["gy"]
    direct = groups > 1 and TPD % groups == 0 and width_parts == 4
    local = kernel_local if direct else plain_local
    placed = (P("gx", "gy"), P("gy", None), P(), P(), P())
    return jax.shard_map(
        local, mesh=mesh, in_specs=placed, out_specs=(P("gx", "gy"), P("gx", "gy")), check_vma=False
    )
```

profile of v0, /device:TPU:0, one launch (start us, length us, event | category | flops | bytes accessed | tf_op | source)
XLA Modules:
  0.0 91.0 jit_solution(4274278369450801882)
XLA Ops:
  0.7 0.7 dynamic_slice.3
  1.4 0.7 broadcast_compare_fusion.1
  2.1 0.7 fusion.10
  2.8 0.1 broadcast_compare_fusion
  2.9 0.1 iota_compare_fusion.3
  2.9 0.5 select_reduce_fusion
  3.4 0.2 select_reduce_fusion.3
  3.6 0.1 select_reduce_fusion.2
  3.7 0.1 select_reduce_fusion.1
  3.8 0.1 reshape.223
  3.9 0.1 reduce_sum.45
  4.0 0.6 reduce_max.9
  6.0 0.1 minimum_add_fusion
  6.0 0.1 add.215
  6.1 82.5 %conditional.1 = (bf16[16,128,512]{2,1,0:T(8,128)(2,1)S(1)}) conditional(s32[]{:T(128)} %clamp.3, (s32[128]{0:T(128)S(1)}, s32[128]{0:T(128)S(1)}, s32[16]{0:T(128)S(1)}, f32[1,128]{1,0:T(1,128)}, bf16[128,16,1024]{2,1,0:T(8,128)(2,1)}, /*index=5*/bf16[1024,2048]{1,0:T(8,128)(2,1)}) %tuple.25, (s32[128]{0:T(128)S(1)}, ...), branch_computations={%region_6.7_spmd, %region_7.8_spmd, %region_8.9_spmd} | conditional | bytes 8 | solution.py:338
  6.1 82.5 %project_and_deal_11.1 = bf16[16,128,512]{2,1,0:T(8,128)(2,1)S(1)} custom-call(s32[128]{0:T(128)S(1)} %get-tuple-element.28.source_ref, s32[128]{0:T(128)S(1)} %get-tuple-element.29.piece_ref, s32[16]{0:T(128)S(1)} %get-tuple-element.42.limit_ref, f32[1,128]{1,0:T(1,128)} %get-tuple-element.43.gain_ref, bf16[128,16,1024]{2,1,0:T(8,128)(2,1)} %get-tuple-element.44.feats_ref, ...), custom_call_target="tpu_custom_call" | custom-call | tf_op jit(solution)/shard_map/cond/branch_0_fun/project_and_deal_11/pallas_call | solution.py:338
  88.7 2.3 %place_tiles.1 = (bf16[2048,256]{1,0:T(8,128)(2,1)}, bf16[2048,256]{1,0:T(8,128)(2,1)}) custom-call(s32[8,16]{1,0:T(8,128)} %deal_ref.1, bf16[16,128,512]{2,1,0:T(8,128)(2,1)S(1)} %get-tuple-element.64.dealt_ref), custom_call_target="tpu_custom_call" | custom-call | tf_op jit(solution)/shard_map/place_tiles/pallas_call | solution.py:345
  (6 shorter events, 0.1 us)
where the time goes:
time: 91.2 us; the launch traced here: 91 us
  Pallas kernels  84.8 us (93%)
  other arithmetic  3.24 us (4%)
  between operations  1.99 us (2%)
    pallas_call x1, Pallas kernels, kernel_local(): lax.switch(branch, [project(size, call) for call, size in enumerate(sizes...  82.5 us
    pallas_call x1, Pallas kernels, kernel_local(): pl.pallas_call(functools.partial(place_kernel, groups, slots), out_shape=...  2.31 us

commit v1 on v0

--- a/solution.py
+++ b/solution.py
@@ -64,6 +64,10 @@
 
 MESH = pl.DeviceIdType.MESH
 PIECE = 16
+SCALES = 8
+STEPS = 32767.0
+LEAST = 1e-30
+LEAD = 3
 
 
 def route(step, me, groups, slots):
@@ -103,8 +107,9 @@
 
 def project_kernel(
     groups, slots, chunks, source_ref, piece_ref, limit_ref, gain_ref, feats_ref, w_ref, dealt_ref,
-    natural, mine, theirs, w_mine, w_theirs, x_out, x_in, packed, done,
-    load_sem, w_load_sem, w_send, w_recv, f_send, f_recv, x_send, x_recv, o_send, o_recv, own_sem,
+    natural, mine, theirs, w_mine, w_theirs, x_out, x_in, x_scale_out, x_scale_in, packed, done,
+    load_sem, w_load_sem, w_send, w_recv, f_send, f_recv, x_send, x_recv, s_send, s_recv,
+    o_send, o_recv, own_sem,
 ):
     me = lax.axis_index("gx")
     place = lax.axis_index("gy")
@@ -164,6 +169,12 @@
             recv_sem=x_recv.at[k], device_id=x_mate, device_id_type=MESH,
         )
 
+    def s_copy(k):
+        return pltpu.make_async_remote_copy(
+            src_ref=x_scale_out.at[k], dst_ref=x_scale_in.at[k], send_sem=s_send.at[k],
+            recv_sem=s_recv.at[k], device_id=x_mate, device_id_type=MESH,
+        )
+
     def o_copy(k, target, landing):
         return pltpu.make_async_remote_copy(
             src_ref=done.at[k], dst_ref=dealt_ref.at[landing], send_sem=o_send.at[k],
@@ -195,33 +206,51 @@
         w_loads[b].wait()
         w_copies[b].wait_recv()
 
-    def outward(k, carry):
+    heads = 2 * share // HD
+
+    def outward(k):
         f_copy(k).wait_recv()
-        x_out[k, :, :share] = partial(k, 0)
-        x_out[k, :, share:] = partial(k, 1)
+        lane = lax.broadcasted_iota(jnp.int32, (TILE, HD), 1)
+        peaks = jnp.zeros((TILE, HD), jnp.float32)
+        for block in range(2):
+            sums = partial(k, block)
+            for h in range(heads // 2):
+                one = sums[:, h * HD : (h + 1) * HD]
+                peak = jnp.maximum(jnp.max(jnp.abs(one), axis=-1, keepdims=True), LEAST)
+                place = block * (heads // 2) + h
+                coded = jnp.round(one * (STEPS / peak)).astype(jnp.int32)
+                x_out[k, :, place * HD : (place + 1) * HD] = coded.astype(jnp.int16)
+                peaks = jnp.where(lane == place, peak, peaks)
+        x_scale_out[k] = jnp.transpose(peaks)[:SCALES]
+        s_copy(k).start()
         x_copy(k).start()
-        return carry
-
-    lax.fori_loop(0, chunks, outward, 0)
-    for b in range(2, 4):
-        w_loads[b].wait()
-        w_copies[b].wait_recv()
+
+    def arrived(j):
+        s_copy(j).wait_recv()
+        peaks = jnp.transpose(jnp.concatenate([x_scale_in[j]] * (HD // SCALES), axis=0))
+        x_copy(j).wait_recv()
+        return [
+            x_in[j, :, h * HD : (h + 1) * HD].astype(jnp.float32)
+            * (peaks[:, h : h + 1] * (1.0 / STEPS))
+            for h in range(heads)
+        ]
 
     def finish(j):
         key_part = partial(j, 2)
         value_part = partial(j, 3)
-        x_copy(j).wait_recv()
-        key_pre = key_part + x_in[j, :, :share]
-        value_pre = value_part + x_in[j, :, share:]
+        other = arrived(j)
         parts = TILE // PIECE
         rows = pl.ds(j * parts, parts)
         for h in range(share // HD):
             head = slice(h * HD, (h + 1) * HD)
-            one = key_pre[:, head]
+            one = key_part[:, head] + other[h]
             mean_square = jnp.mean(one * one, axis=-1, keepdims=True)
             normed = one * lax.rsqrt(mean_square + epsilon) * gain_ref[...]
             packed[rows, :, head] = normed.astype(jnp.bfloat16).reshape(parts, PIECE, HD)
-        packed[rows, :, share:] = value_pre.astype(jnp.bfloat16).reshape(parts, PIECE, share)
+            value_pre = value_part[:, head] + other[share // HD + h]
+            packed[rows, :, share + h * HD : share + (h + 1) * HD] = value_pre.astype(
+                jnp.bfloat16
+            ).reshape(parts, PIECE, HD)
 
     def assemble(k):
         position = lax.broadcasted_iota(jnp.int32, (PIECE, 2 * share), 0)
@@ -237,13 +266,26 @@
         o_copy(k, target, me * slots + cls).start()
         return carry
 
+    def start(k, carry):
+        outward(k)
+        return carry
+
     def inward(k, carry):
         finish(k)
         return dispatch(k, carry)
 
+    def both(k, carry):
+        outward(k)
+        return inward(k - LEAD, carry)
+
     leaving = steps - slots
     together = min(chunks, leaving)
-    lax.fori_loop(0, together, inward, 0)
+    lax.fori_loop(0, LEAD, start, 0)
+    for b in range(2, 4):
+        w_loads[b].wait()
+        w_copies[b].wait_recv()
+    lax.fori_loop(LEAD, chunks, both, 0)
+    lax.fori_loop(chunks - LEAD, together, inward, 0)
     for j in range(together, chunks):
         finish(j)
     if together < leaving:
@@ -263,6 +305,7 @@
     def drain(k, carry):
         f_copy(k).wait_send()
         x_copy(k).wait_send()
+        s_copy(k).wait_send()
         return carry
 
     lax.fori_loop(0, chunks, drain, 0)
@@ -320,12 +363,15 @@
                 pltpu.VMEM((chunks, TILE, width), bf16),
                 pltpu.VMEM((4, width, share), bf16),
                 pltpu.VMEM((4, width, share), bf16),
-                pltpu.VMEM((chunks, TILE, 2 * share), f32),
-                pltpu.VMEM((chunks, TILE, 2 * share), f32),
+                pltpu.VMEM((chunks, TILE, 2 * share), jnp.int16),
+                pltpu.VMEM((chunks, TILE, 2 * share), jnp.int16),
+                pltpu.VMEM((chunks, SCALES, HD), f32),
+                pltpu.VMEM((chunks, SCALES, HD), f32),
                 pltpu.VMEM((chunks * TILE // PIECE, PIECE, 2 * share), bf16),
                 pltpu.VMEM((steps, TILE, 2 * share), bf16),
                 dma, dma((4,)), dma((4,)), dma((4,)), dma((chunks,)), dma((chunks,)),
-                dma((chunks,)), dma((chunks,)), dma((steps,)), dma((steps,)), dma((slots,)),
+                dma((chunks,)), dma((chunks,)), dma((chunks,)), dma((chunks,)),
+                dma((steps,)), dma((steps,)), dma((slots,)),
             ],
             compiler_params=pltpu.CompilerParams(collective_id=call, has_side_effects=True),
             name=f"project_and_deal_{chunks}",

time: 91.2 us -> 75.6 us (0.83)
  Pallas kernels: 84.8 us -> 69.2 us
    pallas_call x1, Pallas kernels: 82.5 us -> 66.9 us  [kernel_local(): lax.switch(branch, [project(size, call) for call, size in enumerate(sizes...]
where the time goes in v1:
time: 75.6 us; the launch traced here: 75.3 us
  Pallas kernels  69.2 us (92%)
  other arithmetic  3.24 us (4%)
  between operations  1.99 us (3%)
  local copies, waits for them, and re-layouts  0.9 us (1%)
    pallas_call x1, Pallas kernels, kernel_local(): lax.switch(branch, [project(size, call) for call, size in enumerate(sizes...  66.9 us
    pallas_call x1, Pallas kernels, kernel_local(): pl.pallas_call(functools.partial(place_kernel, groups, slots), out_shape=...  2.31 us

profile of v1, /device:TPU:0, one launch (start us, length us, event | category | flops | bytes accessed | tf_op | source)
XLA Modules:
  0.0 75.3 jit_solution(12201507374829124938)
XLA Ops:
  0.7 0.7 dynamic_slice.3
  1.4 0.7 broadcast_compare_fusion.1
  2.1 0.7 fusion.10
  2.8 0.1 broadcast_compare_fusion
  2.9 0.1 iota_compare_fusion.3
  2.9 0.5 select_reduce_fusion
  3.4 0.2 select_reduce_fusion.3
  3.6 0.1 select_reduce_fusion.2
  3.7 0.1 select_reduce_fusion.1
  3.8 0.1 reshape.223
  3.9 0.1 reduce_sum.45
  4.0 0.6 reduce_max.9
  6.0 0.1 minimum_add_fusion
  6.0 0.1 add.215
  6.1 66.9 %conditional.1 = (bf16[16,128,512]{2,1,0:T(8,128)(2,1)S(1)}) conditional(s32[]{:T(128)} %clamp.3, (s32[128]{0:T(128)S(1)}, s32[128]{0:T(128)S(1)}, s32[16]{0:T(128)S(1)}, f32[1,128]{1,0:T(1,128)}, bf16[128,16,1024]{2,1,0:T(8,128)(2,1)}, /*index=5*/bf16[1024,2048]{1,0:T(8,128)(2,1)}) %tuple.25, (s32[128]{0:T(128)S(1)}, ...), branch_computations={%region_6.7_spmd, %region_7.8_spmd, %region_8.9_spmd} | conditional | bytes 8 | solution.py:384
  6.1 66.9 %project_and_deal_11.1 = bf16[16,128,512]{2,1,0:T(8,128)(2,1)S(1)} custom-call(s32[128]{0:T(128)S(1)} %get-tuple-element.28.source_ref, s32[128]{0:T(128)S(1)} %get-tuple-element.29.piece_ref, s32[16]{0:T(128)S(1)} %get-tuple-element.42.limit_ref, f32[1,128]{1,0:T(1,128)} %get-tuple-element.43.gain_ref, bf16[128,16,1024]{2,1,0:T(8,128)(2,1)} %get-tuple-element.44.feats_ref, ...), custom_call_target="tpu_custom_call" | custom-call | tf_op jit(solution)/shard_map/cond/branch_0_fun/project_and_deal_11/pallas_call | solution.py:384
  73.0 2.3 %place_tiles.1 = (bf16[2048,256]{1,0:T(8,128)(2,1)}, bf16[2048,256]{1,0:T(8,128)(2,1)}) custom-call(s32[8,16]{1,0:T(8,128)} %deal_ref.1, bf16[16,128,512]{2,1,0:T(8,128)(2,1)S(1)} %get-tuple-element.64.dealt_ref), custom_call_target="tpu_custom_call" | custom-call | tf_op jit(solution)/shard_map/place_tiles/pallas_call | solution.py:391
  (6 shorter events, 0.1 us)

commit v2 on v1

--- a/solution.py
+++ b/solution.py
@@ -63,10 +63,10 @@
 
 
 MESH = pl.DeviceIdType.MESH
-PIECE = 16
 SCALES = 8
 STEPS = 32767.0
 LEAST = 1e-30
+AHEAD = 4
 LEAD = 3
 
 
@@ -79,35 +79,9 @@
     return target, step % slots
 
 
-def tables(me, groups, slots, tile_rows, deal):
-    per_tile = TILE // PIECE
-    step = jnp.arange(TPD, dtype=jnp.int32)
-    target, cls = route(step, me, groups, slots)
-    column = jnp.arange(TPD, dtype=jnp.int32)
-    row = jnp.arange(groups, dtype=jnp.int32)
-    named = deal == (me * TPD + column)[None, :]
-    chosen = (
-        named[None] & (target[:, None] == row)[:, :, None]
-        & (cls[:, None] == column // groups)[:, None, :]
-    )
-    slot = jnp.sum(jnp.where(chosen, column, 0), axis=(1, 2))
-    own_rows = lax.dynamic_slice(tile_rows, (me * TPD,), (TPD,))
-    limit = jnp.sum(jnp.where(slot[:, None] == column[None, :], own_rows[None, :], 0), axis=1)
-    count = jnp.maximum((limit + PIECE - 1) // PIECE, 1)
-    first = jnp.sum(jnp.where(step[None, :] < step[:, None], count[None, :], 0), axis=1)
-    place = jnp.arange(TPD * per_tile, dtype=jnp.int32)[:, None]
-    inside = (first[None, :] <= place) & (place < (first + count)[None, :])
-    source = jnp.sum(
-        jnp.where(inside, slot[None, :] * per_tile + place - first[None, :], 0), axis=1
-    )
-    part = jnp.arange(per_tile, dtype=jnp.int32)[None, :]
-    piece = first[:, None] + jnp.minimum(part, count[:, None] - 1)
-    return source, piece.reshape(-1), limit
-
-
 def project_kernel(
-    groups, slots, chunks, source_ref, piece_ref, limit_ref, gain_ref, feats_ref, w_ref, dealt_ref,
-    natural, mine, theirs, w_mine, w_theirs, x_out, x_in, x_scale_out, x_scale_in, packed, done,
+    groups, slots, rows_ref, deal_ref, gain_ref, feats_ref, w_ref, dealt_ref,
+    natural, mine, theirs, w_mine, w_theirs, x_out, x_in, x_scale_out, x_scale_in, done,
     load_sem, w_load_sem, w_send, w_recv, f_send, f_recv, x_send, x_recv, s_send, s_recv,
     o_send, o_recv, own_sem,
 ):
@@ -120,7 +94,9 @@
     x_mate = (me, other_across * 2 + core)
     share = w_mine.shape[2]
     total = w_ref.shape[1] // 2
+    heads = 2 * share // HD
     steps = groups * slots
+    leaving = steps - slots
 
     def columns(block, of_core):
         chip = other_across if block < 2 else across
@@ -181,21 +157,26 @@
             recv_sem=o_recv.at[landing], device_id=(target, place), device_id_type=MESH,
         )
 
+    def own_tile(k):
+        target, cls = route(k, me, groups, slots)
+        slot = 0
+        for column in range(groups):
+            tile = deal_ref[target, cls * groups + column]
+            slot = jnp.where(tile // TPD == me, tile % TPD, slot)
+        return slot
+
+    def order(k):
+        mine[k] = natural[own_tile(k)]
+        f_copy(k).start()
+
     w_copies[0].start()
     w_copies[1].start()
     load.wait()
-
-    def order(j, carry):
-        for part in range(TILE // PIECE):
-            mine[j, part * PIECE : (part + 1) * PIECE, :] = natural[
-                source_ref[j * (TILE // PIECE) + part]
-            ]
-        f_copy(j).start()
-        return carry
-
-    lax.fori_loop(0, chunks, order, 0)
-    w_copies[2].start()
-    w_copies[3].start()
+    for k in range(AHEAD):
+        order(k)
+        if k == 1:
+            w_copies[2].start()
+            w_copies[3].start()
 
     def partial(k, block):
         return jnp.dot(
@@ -205,8 +186,6 @@
     for b in range(2):
         w_loads[b].wait()
         w_copies[b].wait_recv()
-
-    heads = 2 * share // HD
 
     def outward(k):
         f_copy(k).wait_recv()
@@ -217,85 +196,69 @@
             for h in range(heads // 2):
                 one = sums[:, h * HD : (h + 1) * HD]
                 peak = jnp.maximum(jnp.max(jnp.abs(one), axis=-1, keepdims=True), LEAST)
-                place = block * (heads // 2) + h
+                at = block * (heads // 2) + h
                 coded = jnp.round(one * (STEPS / peak)).astype(jnp.int32)
-                x_out[k, :, place * HD : (place + 1) * HD] = coded.astype(jnp.int16)
-                peaks = jnp.where(lane == place, peak, peaks)
+                x_out[k, :, at * HD : (at + 1) * HD] = coded.astype(jnp.int16)
+                peaks = jnp.where(lane == at, peak, peaks)
         x_scale_out[k] = jnp.transpose(peaks)[:SCALES]
         s_copy(k).start()
         x_copy(k).start()
 
-    def arrived(j):
-        s_copy(j).wait_recv()
-        peaks = jnp.transpose(jnp.concatenate([x_scale_in[j]] * (HD // SCALES), axis=0))
-        x_copy(j).wait_recv()
-        return [
-            x_in[j, :, h * HD : (h + 1) * HD].astype(jnp.float32)
-            * (peaks[:, h : h + 1] * (1.0 / STEPS))
-            for h in range(heads)
-        ]
-
-    def finish(j):
-        key_part = partial(j, 2)
-        value_part = partial(j, 3)
-        other = arrived(j)
-        parts = TILE // PIECE
-        rows = pl.ds(j * parts, parts)
-        for h in range(share // HD):
-            head = slice(h * HD, (h + 1) * HD)
-            one = key_part[:, head] + other[h]
-            mean_square = jnp.mean(one * one, axis=-1, keepdims=True)
-            normed = one * lax.rsqrt(mean_square + epsilon) * gain_ref[...]
-            packed[rows, :, head] = normed.astype(jnp.bfloat16).reshape(parts, PIECE, HD)
-            value_pre = value_part[:, head] + other[share // HD + h]
-            packed[rows, :, share + h * HD : share + (h + 1) * HD] = value_pre.astype(
-                jnp.bfloat16
-            ).reshape(parts, PIECE, HD)
-
-    def assemble(k):
-        position = lax.broadcasted_iota(jnp.int32, (PIECE, 2 * share), 0)
-        limit = limit_ref[k]
-        for part in range(TILE // PIECE):
-            held = packed[piece_ref[k * (TILE // PIECE) + part]]
-            kept = jnp.where(position < limit - part * PIECE, held.astype(jnp.float32), 0.0)
-            done[k, part * PIECE : (part + 1) * PIECE, :] = kept.astype(jnp.bfloat16)
-
-    def dispatch(k, carry):
-        assemble(k)
+    def finish(k):
+        key_part = partial(k, 2)
+        value_part = partial(k, 3)
+        s_copy(k).wait_recv()
+        peaks = jnp.transpose(jnp.concatenate([x_scale_in[k]] * (HD // SCALES), axis=0))
+        x_copy(k).wait_recv()
+        limit = rows_ref[me * TPD + own_tile(k)]
+        kept = lax.broadcasted_iota(jnp.int32, (TILE, HD), 0) < limit
+        for at in range(heads):
+            other = x_in[k, :, at * HD : (at + 1) * HD].astype(jnp.float32)
+            other = other * (peaks[:, at : at + 1] * (1.0 / STEPS))
+            head = at % (heads // 2)
+            part = key_part if at < heads // 2 else value_part
+            one = part[:, head * HD : (head + 1) * HD] + other
+            if at < heads // 2:
+                mean_square = jnp.mean(one * one, axis=-1, keepdims=True)
+                one = one * lax.rsqrt(mean_square + epsilon) * gain_ref[...]
+            done[k, :, at * HD : (at + 1) * HD] = jnp.where(kept, one, 0.0).astype(jnp.bfloat16)
+
+    def inward(k):
+        finish(k)
         target, cls = route(k, me, groups, slots)
         o_copy(k, target, me * slots + cls).start()
-        return carry
-
-    def start(k, carry):
+
+    def opening(k, carry):
+        order(k + AHEAD)
         outward(k)
         return carry
 
-    def inward(k, carry):
-        finish(k)
-        return dispatch(k, carry)
-
-    def both(k, carry):
+    def middle(k, carry):
+        @pl.when(k + AHEAD < steps)
+        def _():
+            order(k + AHEAD)
+
         outward(k)
-        return inward(k - LEAD, carry)
-
-    leaving = steps - slots
-    together = min(chunks, leaving)
-    lax.fori_loop(0, LEAD, start, 0)
+        inward(k - LEAD)
+        return carry
+
+    def closing(k, carry):
+        inward(k)
+        return carry
+
+    lax.fori_loop(0, LEAD, opening, 0)
     for b in range(2, 4):
         w_loads[b].wait()
         w_copies[b].wait_recv()
-    lax.fori_loop(LEAD, chunks, both, 0)
-    lax.fori_loop(chunks - LEAD, together, inward, 0)
-    for j in range(together, chunks):
-        finish(j)
-    if together < leaving:
-        lax.fori_loop(together, leaving, dispatch, 0)
+    lax.fori_loop(LEAD, steps, middle, 0)
+    lax.fori_loop(steps - LEAD, leaving, closing, 0)
     own = []
     for c in range(slots):
-        k = leaving + c
-        assemble(k)
+        finish(leaving + c)
         own.append(
-            pltpu.make_async_copy(done.at[k], dealt_ref.at[me * slots + c], own_sem.at[c])
+            pltpu.make_async_copy(
+                done.at[leaving + c], dealt_ref.at[me * slots + c], own_sem.at[c]
+            )
         )
         own[-1].start()
 
@@ -308,7 +271,7 @@
         s_copy(k).wait_send()
         return carry
 
-    lax.fori_loop(0, chunks, drain, 0)
+    lax.fori_loop(0, steps, drain, 0)
 
     def drain_out(k, carry):
         target, cls = route(k, me, groups, slots)
@@ -316,7 +279,7 @@
         o_copy(k, target, target * slots + cls).wait_recv()
         return carry
 
-    lax.fori_loop(0, steps - slots, drain_out, 0)
+    lax.fori_loop(0, leaving, drain_out, 0)
     for copy in own:
         copy.wait()
 
@@ -351,42 +314,28 @@
     anywhere = pl.BlockSpec(memory_space=pl.ANY)
     dma = pltpu.SemaphoreType.DMA
 
-    def project(chunks, call):
-        return pl.pallas_call(
-            functools.partial(project_kernel, groups, slots, chunks),
-            out_shape=jax.ShapeDtypeStruct((TPD, TILE, 2 * share), bf16),
-            in_specs=[smem, smem, smem, pl.BlockSpec(memory_space=pltpu.VMEM), anywhere, anywhere],
-            out_specs=anywhere,
-            scratch_shapes=[
-                pltpu.VMEM((TPD * TILE // PIECE, PIECE, width), bf16),
-                pltpu.VMEM((chunks, TILE, width), bf16),
-                pltpu.VMEM((chunks, TILE, width), bf16),
-                pltpu.VMEM((4, width, share), bf16),
-                pltpu.VMEM((4, width, share), bf16),
-                pltpu.VMEM((chunks, TILE, 2 * share), jnp.int16),
-                pltpu.VMEM((chunks, TILE, 2 * share), jnp.int16),
-                pltpu.VMEM((chunks, SCALES, HD), f32),
-                pltpu.VMEM((chunks, SCALES, HD), f32),
-                pltpu.VMEM((chunks * TILE // PIECE, PIECE, 2 * share), bf16),
-                pltpu.VMEM((steps, TILE, 2 * share), bf16),
-                dma, dma((4,)), dma((4,)), dma((4,)), dma((chunks,)), dma((chunks,)),
-                dma((chunks,)), dma((chunks,)), dma((chunks,)), dma((chunks,)),
-                dma((steps,)), dma((steps,)), dma((slots,)),
-            ],
-            compiler_params=pltpu.CompilerParams(collective_id=call, has_side_effects=True),
-            name=f"project_and_deal_{chunks}",
-        )
-
-    sizes = (TPD * 11 // 16, TPD * 3 // 4, TPD)
-    pieces = jnp.maximum((tile_rows + PIECE - 1) // PIECE, 1).reshape(groups, TPD)
-    fullest = jnp.max(jnp.sum(pieces, axis=1))
-    branch = sum((fullest > size * (TILE // PIECE)).astype(jnp.int32) for size in sizes[:-1])
-    dealt = lax.switch(
-        branch,
-        [project(size, call) for call, size in enumerate(sizes)],
-        *tables(lax.axis_index("gx"), groups, slots, tile_rows, deal),
-        k_gain.reshape(1, HD), image_feats.reshape(-1, PIECE, width), w_kv,
-    )
+    dealt = pl.pallas_call(
+        functools.partial(project_kernel, groups, slots),
+        out_shape=jax.ShapeDtypeStruct((steps, TILE, 2 * share), bf16),
+        in_specs=[smem, smem, pl.BlockSpec(memory_space=pltpu.VMEM), anywhere, anywhere],
+        out_specs=anywhere,
+        scratch_shapes=[
+            pltpu.VMEM((steps, TILE, width), bf16),
+            pltpu.VMEM((steps, TILE, width), bf16),
+            pltpu.VMEM((steps, TILE, width), bf16),
+            pltpu.VMEM((4, width, share), bf16),
+            pltpu.VMEM((4, width, share), bf16),
+            pltpu.VMEM((steps, TILE, 2 * share), jnp.int16),
+            pltpu.VMEM((steps, TILE, 2 * share), jnp.int16),
+            pltpu.VMEM((steps, SCALES, HD), f32),
+            pltpu.VMEM((steps, SCALES, HD), f32),
+            pltpu.VMEM((steps, TILE, 2 * share), bf16),
+            dma, dma((4,)), dma((4,)), dma((4,)),
+            *[dma((steps,)) for _ in range(8)], dma((slots,)),
+        ],
+        compiler_params=pltpu.CompilerParams(collective_id=0, has_side_effects=True),
+        name="project_and_deal",
+    )(tile_rows, deal, k_gain.reshape(1, HD), image_feats.reshape(steps, TILE, width), w_kv)
     result = jax.ShapeDtypeStruct((TPD * TILE, share), bf16)
     return pl.pallas_call(
         functools.partial(place_kernel, groups, slots),

time: 75.6 us -> 71.2 us (0.942)
  other arithmetic: 3.24 us -> 0 us
  between operations: 1.99 us -> 0.64 us
  Pallas kernels: 69.2 us -> 70.4 us
  local copies, waits for them, and re-layouts: 0.9 us -> 0 us
    reduce_sum x5 -> x0, other arithmetic: 0.96 us -> none  [the longest x1 0.45 us: tables(): slot = jnp.sum(jnp.where(chosen, column, 0), axis=(1, 2))]
    pallas_call x1, Pallas kernels: 2.31 us -> 3.19 us  [kernel_local(): pl.pallas_call(functools.partial(place_kernel, groups, slots), out_shape=...]
    eq x3 -> x0, other arithmetic: 0.84 us -> none  [the longest x1 0.69 us: tables(): named = deal == (me * TPD + column)[None, :]]
where the time goes in v2:
time: 71.2 us; the launch traced here: 71 us
  Pallas kernels  70.4 us (99%)
    pallas_call x1, Pallas kernels, kernel_local(): pl.pallas_call(functools.partial(project_kernel, groups, slots), out_shap...  67.2 us
    pallas_call x1, Pallas kernels, kernel_local(): pl.pallas_call(functools.partial(place_kernel, groups, slots), out_shape=...  3.19 us

profile of v2, /device:TPU:0, one launch (start us, length us, event | category | flops | bytes accessed | tf_op | source)
XLA Modules:
  0.0 71.0 jit_solution(14799794725891827084)
XLA Ops:
  0.6 67.2 %project_and_deal.1.dealt_ref = bf16[16,128,512]{2,1,0:T(8,128)(2,1)} custom-call(s32[128]{0:T(128)} %rows_ref.1, s32[8,16]{1,0:T(8,128)} %deal_ref.3, f32[1,128]{1,0:T(1,128)} %bitcast.3, bf16[16,128,1024]{2,1,0:T(8,128)(2,1)} %bitcast.2, bf16[1024,2048]{1,0:T(8,128)(2,1)} %w_ref.1), custom_call_target="tpu_custom_call" | custom-call | tf_op jit(solution)/shard_map/project_and_deal/pallas_call | solution.py:317
  67.8 3.2 %place_tiles.1 = (bf16[2048,256]{1,0:T(8,128)(2,1)}, bf16[2048,256]{1,0:T(8,128)(2,1)}) custom-call(s32[8,16]{1,0:T(8,128)} %deal_ref.3, bf16[16,128,512]{2,1,0:T(8,128)(2,1)} %project_and_deal.1.dealt_ref), custom_call_target="tpu_custom_call" | custom-call | tf_op jit(solution)/shard_map/place_tiles/pallas_call | solution.py:340

commit v3 on v2

v3 whole, which is shorter than its diff:
```python
import functools

import jax
import jax.numpy as jnp
from jax import lax
from jax.experimental import pallas as pl
from jax.experimental.pallas import tpu as pltpu
from jax.sharding import PartitionSpec as P

HD = 128
TILE = 128
TPD = 16


epsilon = 1e-05


def plain_local(image_feats, w_kv, k_gain, tile_rows, deal):
    local_width = image_feats.shape[1]
    groups = lax.axis_size("gx")
    own_index = lax.axis_index("gx")
    slots = max(1, TPD // groups)
    wanted = lax.dynamic_index_in_dim(deal, own_index, 0, keepdims=False)
    slot_index = jnp.arange(TPD, dtype=jnp.int32)
    slot_class = slot_index // groups
    places = jnp.arange(slots, dtype=jnp.int32)
    class_match = slot_class[None, :] == places[:, None]
    own_tiles = own_index * TPD + slot_index
    sending = deal == own_tiles[None, :]
    send_select = (sending[:, None, :] & class_match[None, :, :]).astype(jnp.bfloat16)
    blocks = image_feats.reshape(TPD, TILE, local_width)
    outgoing = jnp.einsum(
        "dcs,str->dctr", send_select, blocks, preferred_element_type=jnp.float32
    ).astype(jnp.bfloat16)
    incoming = lax.all_to_all(outgoing, "gx", split_axis=0, concat_axis=0, tiled=True)
    sources = jnp.arange(groups, dtype=jnp.int32)
    from_source = (wanted // TPD)[:, None] == sources[None, :]
    take_select = (from_source[:, :, None] & class_match.T[:, None, :]).astype(jnp.bfloat16)
    dealt_tiles = jnp.einsum(
        "snc,nctr->str", take_select, incoming, preferred_element_type=jnp.float32
    ).astype(jnp.bfloat16)
    row_count = TPD * TILE
    dealt_rows = dealt_tiles.reshape(row_count, local_width)
    total_kv = w_kv.shape[1] // 2
    partial_value = jnp.dot(dealt_rows, w_kv, preferred_element_type=jnp.float32)
    projected = lax.psum_scatter(
        partial_value.reshape(row_count, 2, total_kv), "gy", scatter_dimension=2, tiled=True
    )
    share_cols = projected.shape[2]
    key_pre = projected[:, 0, :].reshape(row_count, share_cols // HD, HD)
    value_pre = projected[:, 1, :]
    mean_square = jnp.mean(key_pre * key_pre, axis=-1, keepdims=True)
    normed = (key_pre * lax.rsqrt(mean_square + epsilon) * k_gain).reshape(row_count, share_cols)
    all_tiles = jnp.arange(tile_rows.shape[0], dtype=jnp.int32)
    limits = jnp.sum(
        jnp.where(wanted[:, None] == all_tiles[None, :], tile_rows[None, :], 0), axis=1
    )
    position = jnp.arange(TILE, dtype=jnp.int32)
    valid_rows = (position[None, :] < limits[:, None]).reshape(row_count, 1)
    keys_out = jnp.where(valid_rows, normed, 0.0).astype(jnp.bfloat16)
    values_out = jnp.where(valid_rows, value_pre, 0.0).astype(jnp.bfloat16)
    return (keys_out, values_out)


MESH = pl.DeviceIdType.MESH
SCALES = 8
STEPS = 32767.0
LEAST = 1e-30
AHEAD = 4
LEAD = 2
PARTS = 4


def route(step, me, groups, slots):
    flips = groups - 1 - step // slots
    target, bit = 0, 1
    while bit < groups:
        target += (me // bit + flips // bit) % 2 * bit
        bit *= 2
    return target, step % slots


def project_kernel(
    groups, slots, rows_ref, deal_ref, gain_ref, feats_ref, w_ref, keys_ref, values_ref,
    natural, mine, theirs, w_mine, w_give, w_theirs, x_out, x_in, x_scale_out, x_scale_in,
    done, landed, load_sem, w_load_sem, w_give_sem, w_send, w_recv, f_send, f_recv,
    x_send, x_recv, s_send, s_recv, o_send, o_recv, answer_sem, open_sem,
):
    me = lax.axis_index("gx")
    place = lax.axis_index("gy")
    across = place // 2
    core = place % 2
    other_across, other_core = 1 - across, 1 - core
    core_mate = (me, across * 2 + other_core)
    x_mate = (me, other_across * 2 + core)
    share = w_mine.shape[2]
    total = w_ref.shape[1] // 2
    heads = share // HD
    steps = groups * slots
    leaving = steps - slots

    def columns(block, of_core):
        chip = other_across if block < 2 else across
        first = (block % 2) * total + (chip * 2 + of_core) * share
        return pl.ds(pl.multiple_of(first, 128), share)

    def w_load(b, of_core, into, sem):
        return pltpu.make_async_copy(w_ref.at[:, columns(b, of_core)], into.at[b], sem.at[b])

    load = pltpu.make_async_copy(feats_ref, natural, load_sem)
    w_loads = [w_load(b, core, w_mine, w_load_sem) for b in range(4)]
    w_gives = [w_load(b, other_core, w_give, w_give_sem) for b in range(4)]
    for copy in (*w_gives[:2], load, *w_loads[:2], *w_gives[2:], *w_loads[2:]):
        copy.start()

    barrier = pltpu.get_barrier_semaphore()
    leads = place == 0
    leader = (me, 0)
    knows_leader = (place == 1) | (place == 2)

    @pl.when(~knows_leader)
    def _():
        for mate in (core_mate, x_mate):
            pl.semaphore_signal(barrier, inc=1, device_id=mate, device_id_type=MESH)

    @pl.when(knows_leader)
    def _():
        pl.semaphore_signal(barrier, inc=1, device_id=(me, 3), device_id_type=MESH)

    @pl.when(~leads)
    def _():
        pl.semaphore_wait(barrier, 2)

    @pl.when(knows_leader)
    def _():
        pl.semaphore_signal(answer_sem, inc=1, device_id=leader, device_id_type=MESH)

    @pl.when(leads)
    def _():
        pl.semaphore_wait(answer_sem, 2)
        for ahead in range(1, groups):
            pl.semaphore_signal(
                barrier, inc=1, device_id=((me + ahead) % groups, 0), device_id_type=MESH
            )

    def open_deal():
        pl.semaphore_wait(barrier, groups - 1)
        for mate in range(1, 4):
            pl.semaphore_signal(open_sem, inc=1, device_id=(me, mate), device_id_type=MESH)

    w_copies = [
        pltpu.make_async_remote_copy(
            src_ref=w_give.at[b],
            dst_ref=w_theirs.at[b],
            send_sem=w_send.at[b],
            recv_sem=w_recv.at[b],
            device_id=core_mate,
            device_id_type=MESH,
        )
        for b in range(4)
    ]

    def send_weights(b):
        w_gives[b].wait()
        w_copies[b].start()

    def f_copy(k):
        return pltpu.make_async_remote_copy(
            src_ref=mine.at[k], dst_ref=theirs.at[k], send_sem=f_send.at[k],
            recv_sem=f_recv.at[k], device_id=core_mate, device_id_type=MESH,
        )

    def x_copy(b, k):
        return pltpu.make_async_remote_copy(
            src_ref=x_out.at[b, k], dst_ref=x_in.at[b, k], send_sem=x_send.at[b, k],
            recv_sem=x_recv.at[b, k], device_id=x_mate, device_id_type=MESH,
        )

    def s_copy(b, k):
        return pltpu.make_async_remote_copy(
            src_ref=x_scale_out.at[b, k], dst_ref=x_scale_in.at[b, k], send_sem=s_send.at[b, k],
            recv_sem=s_recv.at[b, k], device_id=x_mate, device_id_type=MESH,
        )

    def o_copy(b, k, target, landing):
        return pltpu.make_async_remote_copy(
            src_ref=done.at[b, k], dst_ref=landed.at[b, landing], send_sem=o_send.at[b, k],
            recv_sem=o_recv.at[b, landing], device_id=(target, place), device_id_type=MESH,
        )

    def own_tile(k):
        target, cls = route(k, me, groups, slots)
        slot = 0
        for column in range(groups):
            tile = deal_ref[target, cls * groups + column]
            slot = jnp.where(tile // TPD == me, tile % TPD, slot)
        return slot

    def order(k):
        mine[k] = natural[own_tile(k)]
        f_copy(k).start()

    send_weights(0)
    load.wait()
    order(0)
    send_weights(1)
    order(1)
    send_weights(2)
    send_weights(3)
    for k in range(2, AHEAD):
        order(k)

    def partial(k, block):
        return jnp.dot(
            mine[k], w_mine[block], preferred_element_type=jnp.float32
        ) + jnp.dot(theirs[k], w_theirs[block], preferred_element_type=jnp.float32)

    def weights_here(b):
        w_loads[b].wait()
        w_copies[b].wait_recv()

    def outward(k, first):
        f_copy(k).wait_recv()
        lane = lax.broadcasted_iota(jnp.int32, (TILE, HD), 1)
        for b in range(2):
            if first:
                weights_here(b)
            sums = partial(k, b)
            peaks = jnp.zeros((TILE, HD), jnp.float32)
            for h in range(heads):
                one = sums[:, h * HD : (h + 1) * HD]
                peak = jnp.maximum(jnp.max(jnp.abs(one), axis=-1, keepdims=True), LEAST)
                coded = jnp.round(one * (STEPS / peak)).astype(jnp.int32)
                x_out[b, k, :, h * HD : (h + 1) * HD] = coded.astype(jnp.int16)
                peaks = jnp.where(lane == h, peak, peaks)
            x_scale_out[b, k] = jnp.transpose(peaks)[:SCALES]
            s_copy(b, k).start()
            x_copy(b, k).start()

    def finish(k, send):
        limit = rows_ref[me * TPD + own_tile(k)]
        kept = lax.broadcasted_iota(jnp.int32, (TILE, HD), 0) < limit
        target, cls = route(k, me, groups, slots)
        for b in range(2):
            part = partial(k, 2 + b)
            s_copy(b, k).wait_recv()
            peaks = jnp.transpose(jnp.concatenate([x_scale_in[b, k]] * (HD // SCALES), axis=0))
            x_copy(b, k).wait_recv()
            for h in range(heads):
                head = slice(h * HD, (h + 1) * HD)
                other = x_in[b, k, :, head].astype(jnp.float32)
                one = part[:, head] + other * (peaks[:, h : h + 1] * (1.0 / STEPS))
                if b == 0:
                    mean_square = jnp.mean(one * one, axis=-1, keepdims=True)
                    one = one * lax.rsqrt(mean_square + epsilon) * gain_ref[...]
                done[b, k, :, head] = jnp.where(kept, one, 0.0).astype(jnp.bfloat16)
            if send:
                o_copy(b, k, target, me * slots + cls).start()
            else:
                landed[b, target * slots + cls] = done[b, k]

    def opening(k, carry):
        order(k + AHEAD)
        outward(k, False)
        return carry

    def middle(k, carry):
        @pl.when(k + AHEAD < steps)
        def _():
            order(k + AHEAD)

        outward(k, False)
        finish(k - LEAD, True)
        return carry

    def closing(k, carry):
        finish(k, True)
        return carry

    outward(0, True)
    pl.when(leads)(open_deal)
    order(AHEAD)
    lax.fori_loop(1, LEAD, opening, 0)
    for b in range(2, 4):
        weights_here(b)

    @pl.when(~leads)
    def _():
        pl.semaphore_wait(open_sem, 1)

    lax.fori_loop(LEAD, steps, middle, 0)
    lax.fori_loop(steps - LEAD, leaving, closing, 0)
    for c in range(slots):
        finish(leaving + c, False)

    for copy in w_copies:
        copy.wait_send()

    def drain(k, carry):
        f_copy(k).wait_send()
        for b in range(2):
            x_copy(b, k).wait_send()
            s_copy(b, k).wait_send()
        return carry

    lax.fori_loop(0, steps, drain, 0)

    def drain_out(k, carry):
        target, cls = route(k, me, groups, slots)
        for b in range(2):
            o_copy(b, k, target, me * slots + cls).wait_send()
            o_copy(b, k, target, target * slots + cls).wait_recv()
        return carry

    lax.fori_loop(0, leaving, drain_out, 0)

    def settle(tile, carry):
        landing = deal_ref[me, tile] // TPD * slots + tile // groups
        rows = pl.ds(pl.multiple_of(tile * TILE, TILE), TILE)
        keys_ref[rows, :] = landed[0, landing]
        values_ref[rows, :] = landed[1, landing]
        return carry

    lax.fori_loop(0, TPD, settle, 0)


def store_kernel(keys_ref, values_ref, keys_out, values_out, sem):
    parts = keys_ref.shape[0] // PARTS
    stores = []
    for which, (source, out) in enumerate(((keys_ref, keys_out), (values_ref, values_out))):
        for part in range(PARTS):
            rows = pl.ds(part * parts, parts)
            stores.append(
                pltpu.make_async_copy(source.at[rows], out.at[rows], sem.at[which, part])
            )
            stores[-1].start()
    for copy in stores:
        copy.wait()


def kernel_local(image_feats, w_kv, k_gain, tile_rows, deal):
    groups = lax.axis_size("gx")
    slots = TPD // groups
    width = image_feats.shape[1]
    share = w_kv.shape[1] // 2 // lax.axis_size("gy")
    steps = TPD
    bf16, f32 = jnp.bfloat16, jnp.float32
    smem = pl.BlockSpec(memory_space=pltpu.SMEM)
    anywhere = pl.BlockSpec(memory_space=pl.ANY)
    dma = pltpu.SemaphoreType.DMA

    tiles = pltpu.VMEM((steps, TILE, width), bf16)
    weights = pltpu.VMEM((4, width, share), bf16)
    codes = pltpu.VMEM((2, steps, TILE, share), jnp.int16)
    scales = pltpu.VMEM((2, steps, SCALES, HD), f32)
    results = pltpu.VMEM((2, steps, TILE, share), bf16)
    result = pltpu.VMEM((TPD * TILE, share), bf16)
    vmem = pl.BlockSpec(memory_space=pltpu.VMEM)
    results = pl.pallas_call(
        functools.partial(project_kernel, groups, slots),
        out_shape=(result, result),
        in_specs=[smem, smem, vmem, anywhere, anywhere],
        out_specs=(vmem, vmem),
        scratch_shapes=[
            tiles, tiles, tiles, weights, weights, weights, codes, codes, scales, scales,
            results, results, dma, dma((4,)), dma((4,)), dma((4,)), dma((4,)),
            dma((steps,)), dma((steps,)), *[dma((2, steps)) for _ in range(6)],
            pltpu.SemaphoreType.REGULAR, pltpu.SemaphoreType.REGULAR,
        ],
        compiler_params=pltpu.CompilerParams(collective_id=0, has_side_effects=True),
        name="project_and_deal",
    )(tile_rows, deal, k_gain.reshape(1, HD), image_feats.reshape(steps, TILE, width), w_kv)
    stored = jax.ShapeDtypeStruct((TPD * TILE, share), bf16)
    return pl.pallas_call(
        store_kernel,
        out_shape=(stored, stored),
        in_specs=[vmem, vmem],
        out_specs=(anywhere, anywhere),
        scratch_shapes=[dma((2, PARTS))],
        name="store_result",
    )(*[pltpu.with_memory_space_constraint(part, pltpu.VMEM) for part in results])


def solution(mesh):
    groups, width_parts = mesh.shape["gx"], mesh.shape["gy"]
    direct = groups > 1 and TPD % groups == 0 and width_parts == 4
    local = kernel_local if direct else plain_local
    placed = (P("gx", "gy"), P("gy", None), P(), P(), P())
    return jax.shard_map(
        local, mesh=mesh, in_specs=placed, out_specs=(P("gx", "gy"), P("gx", "gy")), check_vma=False
    )
```

time: 71.2 us -> 66.9 us (0.940)
  Pallas kernels: 70.4 us -> 66.1 us
    pallas_call x1, Pallas kernels: 67.2 us -> 64.8 us  [kernel_local(): pl.pallas_call(functools.partial(project_kernel, groups, slots), out_shap...]
    pallas_call x1, Pallas kernels: 3.19 us -> 1.38 us  [kernel_local(): pl.pallas_call(store_kernel, out_shape=(stored, stored), in_specs=[vmem,...]
where the time goes in v3:
time: 66.9 us; the launch traced here: 66.8 us
  Pallas kernels  66.1 us (99%)
    pallas_call x1, Pallas kernels, kernel_local(): pl.pallas_call(functools.partial(project_kernel, groups, slots), out_shap...  64.8 us
    pallas_call x1, Pallas kernels, kernel_local(): pl.pallas_call(store_kernel, out_shape=(stored, stored), in_specs=[vmem,...  1.38 us

profile of v3, /device:TPU:0, one launch (start us, length us, event | category | flops | bytes accessed | tf_op | source)
XLA Modules:
  0.0 66.8 jit_solution(13637142810175023385)
XLA Ops:
  0.6 64.8 %project_and_deal.1 = (bf16[2048,256]{1,0:T(8,128)(2,1)S(1)}, bf16[2048,256]{1,0:T(8,128)(2,1)S(1)}) custom-call(s32[128]{0:T(128)} %rows_ref.1, s32[8,16]{1,0:T(8,128)} %deal_ref.1, f32[1,128]{1,0:T(1,128)} %bitcast.3, bf16[16,128,1024]{2,1,0:T(8,128)(2,1)} %bitcast.2, bf16[1024,2048]{1,0:T(8,128)(2,1)} %w_ref.1), custom_call_target="tpu_custom_call" | custom-call | tf_op jit(solution)/shard_map/project_and_deal/pallas_call | solution.py:359
  65.4 1.4 %store_result.1 = (bf16[2048,256]{1,0:T(8,128)(2,1)}, bf16[2048,256]{1,0:T(8,128)(2,1)}) custom-call(bf16[2048,256]{1,0:T(8,128)(2,1)S(1)} %get-tuple-element.4.keys_ref, bf16[2048,256]{1,0:T(8,128)(2,1)S(1)} %get-tuple-element.5.values_ref), custom_call_target="tpu_custom_call" | custom-call | tf_op jit(solution)/shard_map/store_result/pallas_call | solution.py:374

commit v4 on v3

--- a/solution.py
+++ b/solution.py
@@ -63,7 +63,6 @@
 
 
 MESH = pl.DeviceIdType.MESH
-SCALES = 8
 STEPS = 32767.0
 LEAST = 1e-30
 AHEAD = 4
@@ -71,8 +70,20 @@
 PARTS = 4
 
 
+def down(top, bottom):
+    return list(range(top - 1, bottom - 1, -1))
+
+
 def route(step, me, groups, slots):
-    flips = groups - 1 - step // slots
+    turn, quarter = step // slots, groups // 4
+    at_end = (me // quarter) % 3 == 0
+    outer = down(groups, 0)
+    inner = [
+        *down(3 * quarter, quarter), *down(groups, 3 * quarter), *down(quarter, 0)
+    ]
+    flips = 0
+    for at, (far, near) in enumerate(zip(outer, inner)):
+        flips = jnp.where(turn == at, jnp.where(at_end, far, near), flips)
     target, bit = 0, 1
     while bit < groups:
         target += (me // bit + flips // bit) % 2 * bit
@@ -176,10 +187,10 @@
             recv_sem=x_recv.at[b, k], device_id=x_mate, device_id_type=MESH,
         )
 
-    def s_copy(b, k):
+    def s_copy(k):
         return pltpu.make_async_remote_copy(
-            src_ref=x_scale_out.at[b, k], dst_ref=x_scale_in.at[b, k], send_sem=s_send.at[b, k],
-            recv_sem=s_recv.at[b, k], device_id=x_mate, device_id_type=MESH,
+            src_ref=x_scale_out.at[k], dst_ref=x_scale_in.at[k], send_sem=s_send.at[k],
+            recv_sem=s_recv.at[k], device_id=x_mate, device_id_type=MESH,
         )
 
     def o_copy(b, k, target, landing):
@@ -222,19 +233,20 @@
     def outward(k, first):
         f_copy(k).wait_recv()
         lane = lax.broadcasted_iota(jnp.int32, (TILE, HD), 1)
+        peaks = jnp.zeros((TILE, HD), jnp.float32)
         for b in range(2):
             if first:
                 weights_here(b)
             sums = partial(k, b)
-            peaks = jnp.zeros((TILE, HD), jnp.float32)
             for h in range(heads):
                 one = sums[:, h * HD : (h + 1) * HD]
                 peak = jnp.maximum(jnp.max(jnp.abs(one), axis=-1, keepdims=True), LEAST)
                 coded = jnp.round(one * (STEPS / peak)).astype(jnp.int32)
                 x_out[b, k, :, h * HD : (h + 1) * HD] = coded.astype(jnp.int16)
-                peaks = jnp.where(lane == h, peak, peaks)
-            x_scale_out[b, k] = jnp.transpose(peaks)[:SCALES]
-            s_copy(b, k).start()
+                peaks = jnp.where(lane == b * heads + h, peak, peaks)
+            if b == 1:
+                x_scale_out[k] = jnp.transpose(peaks)[: 2 * heads]
+                s_copy(k).start()
             x_copy(b, k).start()
 
     def finish(k, send):
@@ -243,13 +255,15 @@
         target, cls = route(k, me, groups, slots)
         for b in range(2):
             part = partial(k, 2 + b)
-            s_copy(b, k).wait_recv()
-            peaks = jnp.transpose(jnp.concatenate([x_scale_in[b, k]] * (HD // SCALES), axis=0))
+            if b == 0:
+                s_copy(k).wait_recv()
+                repeats = HD // (2 * heads)
+                peaks = jnp.transpose(jnp.concatenate([x_scale_in[k]] * repeats, axis=0))
             x_copy(b, k).wait_recv()
             for h in range(heads):
-                head = slice(h * HD, (h + 1) * HD)
+                head, at = slice(h * HD, (h + 1) * HD), b * heads + h
                 other = x_in[b, k, :, head].astype(jnp.float32)
-                one = part[:, head] + other * (peaks[:, h : h + 1] * (1.0 / STEPS))
+                one = part[:, head] + other * (peaks[:, at : at + 1] * (1.0 / STEPS))
                 if b == 0:
                     mean_square = jnp.mean(one * one, axis=-1, keepdims=True)
                     one = one * lax.rsqrt(mean_square + epsilon) * gain_ref[...]
@@ -298,9 +312,9 @@
 
     def drain(k, carry):
         f_copy(k).wait_send()
+        s_copy(k).wait_send()
         for b in range(2):
             x_copy(b, k).wait_send()
-            s_copy(b, k).wait_send()
         return carry
 
     lax.fori_loop(0, steps, drain, 0)
@@ -352,7 +366,7 @@
     tiles = pltpu.VMEM((steps, TILE, width), bf16)
     weights = pltpu.VMEM((4, width, share), bf16)
     codes = pltpu.VMEM((2, steps, TILE, share), jnp.int16)
-    scales = pltpu.VMEM((2, steps, SCALES, HD), f32)
+    scales = pltpu.VMEM((steps, 2 * share // HD, HD), f32)
     results = pltpu.VMEM((2, steps, TILE, share), bf16)
     result = pltpu.VMEM((TPD * TILE, share), bf16)
     vmem = pl.BlockSpec(memory_space=pltpu.VMEM)
@@ -364,7 +378,8 @@
         scratch_shapes=[
             tiles, tiles, tiles, weights, weights, weights, codes, codes, scales, scales,
             results, results, dma, dma((4,)), dma((4,)), dma((4,)), dma((4,)),
-            dma((steps,)), dma((steps,)), *[dma((2, steps)) for _ in range(6)],
+            dma((steps,)), dma((steps,)), dma((2, steps)), dma((2, steps)),
+            dma((steps,)), dma((steps,)), dma((2, steps)), dma((2, steps)),
             pltpu.SemaphoreType.REGULAR, pltpu.SemaphoreType.REGULAR,
         ],
         compiler_params=pltpu.CompilerParams(collective_id=0, has_side_effects=True),
@@ -383,7 +398,7 @@
 
 def solution(mesh):
     groups, width_parts = mesh.shape["gx"], mesh.shape["gy"]
-    direct = groups > 1 and TPD % groups == 0 and width_parts == 4
+    direct = groups % 4 == 0 and TPD % groups == 0 and width_parts == 4
     local = kernel_local if direct else plain_local
     placed = (P("gx", "gy"), P("gy", None), P(), P(), P())
     return jax.shard_map(

time: 66.9 us -> 62.6 us (0.936)
  the two profiles are of different devices: /device:TPU:0 before, /device:TPU:8 now
where the time goes in v4:
time: 62.6 us; the launch traced here: 62.4 us
  Pallas kernels  61.8 us (99%)
  between operations  0.64 us (1%)
    pallas_call x1, Pallas kernels, kernel_local(): pl.pallas_call(functools.partial(project_kernel, groups, slots), out_shap...  60.4 us
    pallas_call x1, Pallas kernels, kernel_local(): pl.pallas_call(store_kernel, out_shape=(stored, stored), in_specs=[vmem,...  1.38 us

profile of v4, /device:TPU:8, one launch (start us, length us, event | category | flops | bytes accessed | tf_op | source)
XLA Modules:
  0.0 62.4 jit_solution(6754801505610635866)
XLA Ops:
  0.6 60.4 %project_and_deal.1 = (bf16[2048,256]{1,0:T(8,128)(2,1)S(1)}, bf16[2048,256]{1,0:T(8,128)(2,1)S(1)}) custom-call(s32[128]{0:T(128)} %rows_ref.1, s32[8,16]{1,0:T(8,128)} %deal_ref.1, f32[1,128]{1,0:T(1,128)} %bitcast.3, bf16[16,128,1024]{2,1,0:T(8,128)(2,1)} %bitcast.2, bf16[1024,2048]{1,0:T(8,128)(2,1)} %w_ref.1), custom_call_target="tpu_custom_call" | custom-call | tf_op jit(solution)/shard_map/project_and_deal/pallas_call | solution.py:373
  61.1 1.4 %store_result.1 = (bf16[2048,256]{1,0:T(8,128)(2,1)}, bf16[2048,256]{1,0:T(8,128)(2,1)}) custom-call(bf16[2048,256]{1,0:T(8,128)(2,1)S(1)} %get-tuple-element.4.keys_ref, bf16[2048,256]{1,0:T(8,128)(2,1)S(1)} %get-tuple-element.5.values_ref), custom_call_target="tpu_custom_call" | custom-call | tf_op jit(solution)/shard_map/store_result/pallas_call | solution.py:389

commit v5 on v4

--- a/solution.py
+++ b/solution.py
@@ -95,7 +95,7 @@
     groups, slots, rows_ref, deal_ref, gain_ref, feats_ref, w_ref, keys_ref, values_ref,
     natural, mine, theirs, w_mine, w_give, w_theirs, x_out, x_in, x_scale_out, x_scale_in,
     done, landed, load_sem, w_load_sem, w_give_sem, w_send, w_recv, f_send, f_recv,
-    x_send, x_recv, s_send, s_recv, o_send, o_recv, answer_sem, open_sem,
+    x_send, x_recv, s_send, s_recv, o_send, o_recv, core_sem, x_sem, open_sem,
 ):
     me = lax.axis_index("gx")
     place = lax.axis_index("gy")
@@ -118,46 +118,58 @@
     def w_load(b, of_core, into, sem):
         return pltpu.make_async_copy(w_ref.at[:, columns(b, of_core)], into.at[b], sem.at[b])
 
-    load = pltpu.make_async_copy(feats_ref, natural, load_sem)
+    loads = [
+        pltpu.make_async_copy(
+            feats_ref.at[pl.ds(c * groups, groups)], natural[c], load_sem.at[c]
+        )
+        for c in range(slots)
+    ]
     w_loads = [w_load(b, core, w_mine, w_load_sem) for b in range(4)]
     w_gives = [w_load(b, other_core, w_give, w_give_sem) for b in range(4)]
-    for copy in (*w_gives[:2], load, *w_loads[:2], *w_gives[2:], *w_loads[2:]):
+    for copy in (w_gives[0], loads[0], w_gives[1], w_loads[0], *loads[1:], w_loads[1]):
+        copy.start()
+    for copy in (*w_gives[2:], *w_loads[2:]):
         copy.start()
 
     barrier = pltpu.get_barrier_semaphore()
     leads = place == 0
-    leader = (me, 0)
-    knows_leader = (place == 1) | (place == 2)
-
-    @pl.when(~knows_leader)
+    answers = place == 2
+
+    def greet(sem, mate):
+        pl.semaphore_signal(sem, inc=1, device_id=mate, device_id_type=MESH)
+
+    @pl.when(core == 0)
     def _():
-        for mate in (core_mate, x_mate):
-            pl.semaphore_signal(barrier, inc=1, device_id=mate, device_id_type=MESH)
-
-    @pl.when(knows_leader)
+        greet(barrier, core_mate)
+        pl.semaphore_wait(core_sem, 1)
+
+    @pl.when(core == 1)
     def _():
-        pl.semaphore_signal(barrier, inc=1, device_id=(me, 3), device_id_type=MESH)
-
-    @pl.when(~leads)
-    def _():
-        pl.semaphore_wait(barrier, 2)
-
-    @pl.when(knows_leader)
-    def _():
-        pl.semaphore_signal(answer_sem, inc=1, device_id=leader, device_id_type=MESH)
-
-    @pl.when(leads)
-    def _():
-        pl.semaphore_wait(answer_sem, 2)
-        for ahead in range(1, groups):
-            pl.semaphore_signal(
-                barrier, inc=1, device_id=((me + ahead) % groups, 0), device_id_type=MESH
-            )
+        pl.semaphore_wait(barrier, 1)
+        greet(core_sem, core_mate)
+
+    pl.when(leads)(lambda: greet(barrier, x_mate))
+
+    def answer_x():
+        pl.semaphore_wait(barrier, 1)
+        greet(x_sem, x_mate)
+        greet(x_sem, core_mate)
+
+    def meet_x():
+        @pl.when(~answers)
+        def _():
+            pl.semaphore_wait(x_sem, 1)
+
+        @pl.when(leads)
+        def _():
+            greet(x_sem, core_mate)
+            for ahead in range(1, groups):
+                greet(barrier, ((me + ahead) % groups, 0))
 
     def open_deal():
         pl.semaphore_wait(barrier, groups - 1)
         for mate in range(1, 4):
-            pl.semaphore_signal(open_sem, inc=1, device_id=(me, mate), device_id_type=MESH)
+            greet(open_sem, (me, mate))
 
     w_copies = [
         pltpu.make_async_remote_copy(
@@ -199,27 +211,40 @@
             recv_sem=o_recv.at[b, landing], device_id=(target, place), device_id_type=MESH,
         )
 
-    def own_tile(k):
+    def own_column(k):
         target, cls = route(k, me, groups, slots)
-        slot = 0
+        own = 0
         for column in range(groups):
-            tile = deal_ref[target, cls * groups + column]
-            slot = jnp.where(tile // TPD == me, tile % TPD, slot)
-        return slot
+            named = deal_ref[target, cls * groups + column]
+            own = jnp.where(named // TPD == me, column, own)
+        return own
 
     def order(k):
-        mine[k] = natural[own_tile(k)]
+        own = own_column(k)
+        if isinstance(k, int):
+            mine[k] = natural[k % slots][own]
+        else:
+            for cls in range(slots):
+
+                @pl.when(k % slots == cls)
+                def _():
+                    mine[k] = natural[cls][own]
+
         f_copy(k).start()
 
     send_weights(0)
-    load.wait()
+    loads[0].wait()
     order(0)
     send_weights(1)
+    pl.when(answers)(answer_x)
+    for copy in loads[1:]:
+        copy.wait()
     order(1)
     send_weights(2)
     send_weights(3)
     for k in range(2, AHEAD):
         order(k)
+    meet_x()
 
     def partial(k, block):
         return jnp.dot(
@@ -250,9 +275,9 @@
             x_copy(b, k).start()
 
     def finish(k, send):
-        limit = rows_ref[me * TPD + own_tile(k)]
+        target, cls = route(k, me, groups, slots)
+        limit = rows_ref[me * TPD + cls * groups + own_column(k)]
         kept = lax.broadcasted_iota(jnp.int32, (TILE, HD), 0) < limit
-        target, cls = route(k, me, groups, slots)
         for b in range(2):
             part = partial(k, 2 + b)
             if b == 0:
@@ -284,6 +309,11 @@
             order(k + AHEAD)
 
         outward(k, False)
+
+        @pl.when(~leads & (k == LEAD))
+        def _():
+            pl.semaphore_wait(open_sem, 1)
+
         finish(k - LEAD, True)
         return carry
 
@@ -292,16 +322,11 @@
         return carry
 
     outward(0, True)
-    pl.when(leads)(open_deal)
     order(AHEAD)
     lax.fori_loop(1, LEAD, opening, 0)
+    pl.when(leads)(open_deal)
     for b in range(2, 4):
         weights_here(b)
-
-    @pl.when(~leads)
-    def _():
-        pl.semaphore_wait(open_sem, 1)
-
     lax.fori_loop(LEAD, steps, middle, 0)
     lax.fori_loop(steps - LEAD, leaving, closing, 0)
     for c in range(slots):
@@ -376,11 +401,12 @@
         in_specs=[smem, smem, vmem, anywhere, anywhere],
         out_specs=(vmem, vmem),
         scratch_shapes=[
-            tiles, tiles, tiles, weights, weights, weights, codes, codes, scales, scales,
-            results, results, dma, dma((4,)), dma((4,)), dma((4,)), dma((4,)),
+            [pltpu.VMEM((groups, TILE, width), bf16)] * slots, tiles, tiles,
+            weights, weights, weights, codes, codes, scales, scales,
+            results, results, dma((slots,)), dma((4,)), dma((4,)), dma((4,)), dma((4,)),
             dma((steps,)), dma((steps,)), dma((2, steps)), dma((2, steps)),
             dma((steps,)), dma((steps,)), dma((2, steps)), dma((2, steps)),
-            pltpu.SemaphoreType.REGULAR, pltpu.SemaphoreType.REGULAR,
+            *[pltpu.SemaphoreType.REGULAR] * 3,
         ],
         compiler_params=pltpu.CompilerParams(collective_id=0, has_side_effects=True),
         name="project_and_deal",

time: 62.6 us -> 61.4 us (0.981)
  Pallas kernels: 61.8 us -> 60.6 us
    pallas_call x1, Pallas kernels: 60.4 us -> 59.3 us  [kernel_local(): pl.pallas_call(functools.partial(project_kernel, groups, slots), out_shap...]
where the time goes in v5:
time: 61.4 us; the launch traced here: 61.3 us
  Pallas kernels  60.6 us (99%)
  between operations  0.64 us (1%)
    pallas_call x1, Pallas kernels, kernel_local(): pl.pallas_call(functools.partial(project_kernel, groups, slots), out_shap...  59.3 us
    pallas_call x1, Pallas kernels, kernel_local(): pl.pallas_call(store_kernel, out_shape=(stored, stored), in_specs=[vmem,...  1.38 us

profile of v5, /device:TPU:8, one launch (start us, length us, event | category | flops | bytes accessed | tf_op | source)
XLA Modules:
  0.0 61.3 jit_solution(3124067354859456248)
XLA Ops:
  0.6 59.3 %project_and_deal.1 = (bf16[2048,256]{1,0:T(8,128)(2,1)S(1)}, bf16[2048,256]{1,0:T(8,128)(2,1)S(1)}) custom-call(s32[128]{0:T(128)} %rows_ref.1, s32[8,16]{1,0:T(8,128)} %deal_ref.1, f32[1,128]{1,0:T(1,128)} %bitcast.3, bf16[16,128,1024]{2,1,0:T(8,128)(2,1)} %bitcast.2, bf16[1024,2048]{1,0:T(8,128)(2,1)} %w_ref.1), custom_call_target="tpu_custom_call" | custom-call | tf_op jit(solution)/shard_map/project_and_deal/pallas_call | solution.py:398
  59.9 1.4 %store_result.1 = (bf16[2048,256]{1,0:T(8,128)(2,1)}, bf16[2048,256]{1,0:T(8,128)(2,1)}) custom-call(bf16[2048,256]{1,0:T(8,128)(2,1)S(1)} %get-tuple-element.4.keys_ref, bf16[2048,256]{1,0:T(8,128)(2,1)S(1)} %get-tuple-element.5.values_ref), custom_call_target="tpu_custom_call" | custom-call | tf_op jit(solution)/shard_map/store_result/pallas_call | solution.py:415

commit v6 on v5

--- a/solution.py
+++ b/solution.py
@@ -329,29 +329,34 @@
         weights_here(b)
     lax.fori_loop(LEAD, steps, middle, 0)
     lax.fori_loop(steps - LEAD, leaving, closing, 0)
-    for c in range(slots):
-        finish(leaving + c, False)
-
     for copy in w_copies:
         copy.wait_send()
 
-    def drain(k, carry):
+    def sent(k, carry):
         f_copy(k).wait_send()
         s_copy(k).wait_send()
         for b in range(2):
             x_copy(b, k).wait_send()
         return carry
 
-    lax.fori_loop(0, steps, drain, 0)
-
-    def drain_out(k, carry):
-        target, cls = route(k, me, groups, slots)
+    def dealt(k, carry):
         for b in range(2):
-            o_copy(b, k, target, me * slots + cls).wait_send()
-            o_copy(b, k, target, target * slots + cls).wait_recv()
-        return carry
-
-    lax.fori_loop(0, leaving, drain_out, 0)
+            o_copy(b, k, me, 0).wait_send()
+        return carry
+
+    def arrived(ahead, carry):
+        source = (me + ahead) % groups
+        for cls in range(slots):
+            for b in range(2):
+                o_copy(b, 0, source, source * slots + cls).wait_recv()
+        return carry
+
+    lax.fori_loop(0, leaving, sent, 0)
+    for c in range(slots):
+        finish(leaving + c, False)
+    lax.fori_loop(leaving, steps, sent, 0)
+    lax.fori_loop(0, leaving, dealt, 0)
+    lax.fori_loop(1, groups, arrived, 0)
 
     def settle(tile, carry):
         landing = deal_ref[me, tile] // TPD * slots + tile // groups
@@ -360,7 +365,7 @@
         values_ref[rows, :] = landed[1, landing]
         return carry
 
-    lax.fori_loop(0, TPD, settle, 0)
+    lax.fori_loop(0, TPD, settle, 0, unroll=16)
 
 
 def store_kernel(keys_ref, values_ref, keys_out, values_out, sem):

time: 61.4 us -> 61.3 us (level)
  no operation moved by 1% of the time
where the time goes in v6:
time: 61.3 us; the launch traced here: 61.1 us
  Pallas kernels  60.5 us (99%)
  between operations  0.64 us (1%)
    pallas_call x1, Pallas kernels, kernel_local(): pl.pallas_call(functools.partial(project_kernel, groups, slots), out_shap...  59.1 us
    pallas_call x1, Pallas kernels, kernel_local(): pl.pallas_call(store_kernel, out_shape=(stored, stored), in_specs=[vmem,...  1.38 us

profile of v6, /device:TPU:8, one launch (start us, length us, event | category | flops | bytes accessed | tf_op | source)
XLA Modules:
  0.0 61.1 jit_solution(6137967710268896213)
XLA Ops:
  0.6 59.1 %project_and_deal.1 = (bf16[2048,256]{1,0:T(8,128)(2,1)S(1)}, bf16[2048,256]{1,0:T(8,128)(2,1)S(1)}) custom-call(s32[128]{0:T(128)} %rows_ref.1, s32[8,16]{1,0:T(8,128)} %deal_ref.1, f32[1,128]{1,0:T(1,128)} %bitcast.3, bf16[16,128,1024]{2,1,0:T(8,128)(2,1)} %bitcast.2, bf16[1024,2048]{1,0:T(8,128)(2,1)} %w_ref.1), custom_call_target="tpu_custom_call" | custom-call | tf_op jit(solution)/shard_map/project_and_deal/pallas_call | solution.py:403
  59.8 1.4 %store_result.1 = (bf16[2048,256]{1,0:T(8,128)(2,1)}, bf16[2048,256]{1,0:T(8,128)(2,1)}) custom-call(bf16[2048,256]{1,0:T(8,128)(2,1)S(1)} %get-tuple-element.4.keys_ref, bf16[2048,256]{1,0:T(8,128)(2,1)S(1)} %get-tuple-element.5.values_ref), custom_call_target="tpu_custom_call" | custom-call | tf_op jit(solution)/shard_map/store_result/pallas_call | solution.py:420

commit v7 on v6

--- a/solution.py
+++ b/solution.py
@@ -126,7 +126,7 @@
     ]
     w_loads = [w_load(b, core, w_mine, w_load_sem) for b in range(4)]
     w_gives = [w_load(b, other_core, w_give, w_give_sem) for b in range(4)]
-    for copy in (w_gives[0], loads[0], w_gives[1], w_loads[0], *loads[1:], w_loads[1]):
+    for copy in (loads[0], w_gives[0], w_gives[1], w_loads[0], *loads[1:], w_loads[1]):
         copy.start()
     for copy in (*w_gives[2:], *w_loads[2:]):
         copy.start()
@@ -308,13 +308,12 @@
         def _():
             order(k + AHEAD)
 
-        outward(k, False)
-
         @pl.when(~leads & (k == LEAD))
         def _():
             pl.semaphore_wait(open_sem, 1)
 
         finish(k - LEAD, True)
+        outward(k, False)
         return carry
 
     def closing(k, carry):

time: 61.3 us -> 61.1 us (level)
  no operation moved by 1% of the time
where the time goes in v7:
time: 61.1 us; the launch traced here: 60.9 us
  Pallas kernels  60.3 us (99%)
  between operations  0.64 us (1%)
    pallas_call x1, Pallas kernels, kernel_local(): pl.pallas_call(functools.partial(project_kernel, groups, slots), out_shap...  58.9 us
    pallas_call x1, Pallas kernels, kernel_local(): pl.pallas_call(store_kernel, out_shape=(stored, stored), in_specs=[vmem,...  1.38 us

profile of v7, /device:TPU:8, one launch (start us, length us, event | category | flops | bytes accessed | tf_op | source)
XLA Modules:
  0.0 60.9 jit_solution(14085886931166149292)
XLA Ops:
  0.6 58.9 %project_and_deal.1 = (bf16[2048,256]{1,0:T(8,128)(2,1)S(1)}, bf16[2048,256]{1,0:T(8,128)(2,1)S(1)}) custom-call(s32[128]{0:T(128)} %rows_ref.1, s32[8,16]{1,0:T(8,128)} %deal_ref.1, f32[1,128]{1,0:T(1,128)} %bitcast.3, bf16[16,128,1024]{2,1,0:T(8,128)(2,1)} %bitcast.2, bf16[1024,2048]{1,0:T(8,128)(2,1)} %w_ref.1), custom_call_target="tpu_custom_call" | custom-call | tf_op jit(solution)/shard_map/project_and_deal/pallas_call | solution.py:402
  59.5 1.4 %store_result.1 = (bf16[2048,256]{1,0:T(8,128)(2,1)}, bf16[2048,256]{1,0:T(8,128)(2,1)}) custom-call(bf16[2048,256]{1,0:T(8,128)(2,1)S(1)} %get-tuple-element.4.keys_ref, bf16[2048,256]{1,0:T(8,128)(2,1)S(1)} %get-tuple-element.5.values_ref), custom_call_target="tpu_custom_call" | custom-call | tf_op jit(solution)/shard_map/store_result/pallas_call | solution.py:419

commit v8 on v7

--- a/solution.py
+++ b/solution.py
@@ -65,7 +65,7 @@
 MESH = pl.DeviceIdType.MESH
 STEPS = 32767.0
 LEAST = 1e-30
-AHEAD = 4
+AHEAD = 2
 LEAD = 2
 PARTS = 4
 

time: 61.1 us -> 61 us (level)
  no operation moved by 1% of the time
where the time goes in v8:
time: 61 us; the launch traced here: 60.9 us
  Pallas kernels  60.2 us (99%)
  between operations  0.64 us (1%)
    pallas_call x1, Pallas kernels, kernel_local(): pl.pallas_call(functools.partial(project_kernel, groups, slots), out_shap...  58.8 us
    pallas_call x1, Pallas kernels, kernel_local(): pl.pallas_call(store_kernel, out_shape=(stored, stored), in_specs=[vmem,...  1.38 us

profile of v8, /device:TPU:8, one launch (start us, length us, event | category | flops | bytes accessed | tf_op | source)
XLA Modules:
  0.0 60.9 jit_solution(17752871280183093385)
XLA Ops:
  0.6 58.8 %project_and_deal.1 = (bf16[2048,256]{1,0:T(8,128)(2,1)S(1)}, bf16[2048,256]{1,0:T(8,128)(2,1)S(1)}) custom-call(s32[128]{0:T(128)} %rows_ref.1, s32[8,16]{1,0:T(8,128)} %deal_ref.1, f32[1,128]{1,0:T(1,128)} %bitcast.3, bf16[16,128,1024]{2,1,0:T(8,128)(2,1)} %bitcast.2, bf16[1024,2048]{1,0:T(8,128)(2,1)} %w_ref.1), custom_call_target="tpu_custom_call" | custom-call | tf_op jit(solution)/shard_map/project_and_deal/pallas_call | solution.py:402
  59.5 1.4 %store_result.1 = (bf16[2048,256]{1,0:T(8,128)(2,1)}, bf16[2048,256]{1,0:T(8,128)(2,1)}) custom-call(bf16[2048,256]{1,0:T(8,128)(2,1)S(1)} %get-tuple-element.4.keys_ref, bf16[2048,256]{1,0:T(8,128)(2,1)S(1)} %get-tuple-element.5.values_ref), custom_call_target="tpu_custom_call" | custom-call | tf_op jit(solution)/shard_map/store_result/pallas_call | solution.py:419
